TPU v7x, 32 devices: a whole 2x2x4 slice. The times are simulated.
32 devices in a mesh: row: 8 (over z, core), col: 4 (over y, x).
Axes of the slice: x: 2, y: 2, z: 4, core: 2. Of those that a mesh axis runs over, the one named last changes fastest.
Arguments:
- matrix: float32 [1728, 65536], P('row', 'col'), may hold values from -6 to 6
- range_basis: float32 [1728, 384], P('col', 'row'), may hold values from -0.21875 to 0.21875
Outputs:
- projected: float32 [384, 65536], P('row')
All inputs are finite; a program needn't handle non-finite values.
Results may differ from a plain program's by a relative error of at most 0.000071.
Values sent between devices are 32-bit elements; how exact they have to be, the bound alone decides.
A program may use at most 128 MiB of HBM per device.

v0:
```python
import jax
import jax.numpy as jnp
from jax import lax
from jax.sharding import PartitionSpec as P


def project(left, right):
    return lax.dot_general(
        left,
        right,
        (((0,), (0,)), ((), ())),
        precision=lax.Precision.HIGHEST,
        preferred_element_type=jnp.float32,
    )


def per_device(matrix, range_basis):
    row_panel = lax.all_gather(range_basis, "col", axis=0, tiled=True)
    local_basis = lax.all_to_all(row_panel, "row", split_axis=0, concat_axis=1, tiled=True)
    owned_rows = lax.psum_scatter(
        project(local_basis, matrix), "row", scatter_dimension=0, tiled=True
    )
    return lax.all_gather(owned_rows, "col", axis=1, tiled=True)


def solution(mesh):
    in_specs = (P("row", "col"), P("col", "row"))
    out_specs = P("row", None)
    return jax.shard_map(
        per_device, mesh=mesh, in_specs=in_specs, out_specs=out_specs, check_vma=False
    )
```

profile of v0, /device:TPU:0, one launch (start us, length us, event | category | flops | bytes accessed | tf_op | source)
XLA Modules:
  0.0 446.0 jit_solution(2097924577313517717)
XLA Ops:
  6.5 0.0 reduce-scatter.2.cloned.1.call-start
  6.5 11.3 %all-gather = f32[4,432,48]{1,2,0:T(8,128)S(1)} all-gather(f32[1,432,48]{1,2,0:T(8,128)} %bitcast.9), channel_id=1, replica_groups=mesh['row'=8,'col'=4] {'col'}, dimensions={0}, use_global_device_ids=true | all-gather | bytes 414720 | tf_op jit(solution)/shard_map/all_gather | solution.py:18
  17.9 0.3 copy.5
  18.1 0.2 all_to_all.14
  18.3 0.1 copy.6
  18.5 17.2 %all_to_all.19 = f32[8,216,48]{1,2,0:T(8,128)S(1)} all-to-all(f32[8,216,48]{1,2,0:T(8,128)S(1)} %copy.6), channel_id=1, replica_groups=mesh['row'=8,'col'=4] {'row'}, dimensions={0} | all-to-all | bytes 663552 | tf_op jit(solution)/shard_map/all_to_all | solution.py:19
  35.7 25.4 %fusion = f32[384,16384]{1,0:T(8,128)} fusion(f32[216,384]{0,1:T(8,128)S(1)} %bitcast.8, f32[216,16384]{1,0:T(8,128)} %param.2), kind=kOutput, calls=%fused_computation | convolution fusion | flops 16307453952 | bytes 39653376 | tf_op jit(solution)/shard_map/dot_general | solution.py:8
  61.1 0.0 reduce-scatter.2.cloned.1.call-update
  61.1 0.0 all-gather.3.cloned.1.call-start
  61.1 245.2 %reduce-scatter.2.cloned.1.call-done = f32[48,16384]{1,0:T(8,128)} async-done(((f32[384,16384]{1,0:T(8,128)}), f32[48,16384]{1,0:T(8,128)}) %reduce-scatter.2.cloned.1.call-update) | async-done | bytes 3145744 | tf_op jit(solution)/shard_map/reduce_scatter | solution.py:20
  306.3 0.0 all-gather.3.cloned.1.call-update
  306.3 122.7 %all-gather.3.cloned.1.call-done = f32[48,65536]{1,0:T(8,128)} async-done(((f32[48,16384]{1,0:T(8,128)}), f32[48,65536]{1,0:T(8,128)}) %all-gather.3.cloned.1.call-update) | async-done | bytes 12582928 | tf_op jit(solution)/shard_map/all_gather | solution.py:23
  429.0 10.2 %copy.8 = f32[48,65536]{1,0:T(8,128)} copy(f32[48,65536]{1,0:T(8,128)} %all-gather.3.cloned.1.call-done) | data formatting | bytes 25165824
Async XLA Ops:
  6.5 299.8 %reduce-scatter.2.cloned.1.call-start = ((), (), s32[]{:S(2)}) async-start(), calls=%async_computation.2 | async-start | bytes 28311552 | tf_op jit(solution)/shard_map/reduce_scatter | solution.py:20
  61.1 367.9 %all-gather.3.cloned.1.call-start = ((), (), s32[]{:S(2)}) async-start(), calls=%async_computation.3 | async-start | bytes 15728640 | tf_op jit(solution)/shard_map/all_gather | solution.py:23
Sparse Core Ops, SparseCore 0:
  61.2 245.0 reduce-scatter.1
  308.1 120.8 all-gather.2
where the time goes:
time: 446 us
  waiting for transfers between devices  368 us (83%)
  blocking collectives  28.5 us (6%)
  matrix products  25.4 us (6%)
  between operations  13.4 us (3%)
  local copies, waits for them, and re-layouts  10.8 us (2%)
    reduce_scatter x1, waiting for transfers between devices, per_device(): lax.psum_scatter(project(local_basis, matrix), 'row', scatter_dimension=0...  245 us
    all_gather x1, waiting for transfers between devices, per_device(): return lax.all_gather(owned_rows, 'col', axis=1, tiled=True)  123 us
    dot_general x1, matrix products, project(): lax.dot_general(left, right, (((0,), (0,)), ((), ())), precision=lax.Prec...  25.4 us
    all_to_all x1, blocking collectives, per_device(): lax.all_to_all(row_panel, 'row', split_axis=0, concat_axis=1, tiled=True)  17.2 us
    all_gather x1, blocking collectives, per_device(): row_panel = lax.all_gather(range_basis, 'col', axis=0, tiled=True)  11.3 us
    unnamed x1, local copies, waits for them, and re-layouts  10.2 us
  transfers between devices with their start and end apart: 2, of which 2 were waited for; matrix products, arithmetic and copies ran while one was open for 0% of the time, Pallas kernels for 0%

commit v1 on v0

v1 whole, which is shorter than its diff:
```python
import jax
import jax.numpy as jnp
from jax import lax
from jax.experimental import pallas as pl
from jax.experimental.pallas import tpu as pltpu
from jax.sharding import PartitionSpec as P

MESH = pl.DeviceIdType.MESH
CHUNKS = 16
CORES = 2


def split_parts(value):
    high = value.astype(jnp.bfloat16)
    return high, (value - high.astype(jnp.float32)).astype(jnp.bfloat16)


def kernel(
    chips, cols, basis_ref, matrix_ref, out_ref, basis, halves, rows, part, sums,
    basis_send, basis_recv, rows_local, rows_send, rows_recv, sum_send, sum_recv, out_send, out_recv,
):
    row, col = lax.axis_index("row"), lax.axis_index("col")
    chip, core = row // CORES, row % CORES
    vectors = basis_ref.shape[0]
    depth = matrix_ref.shape[0]
    chunks, _, width = rows.shape
    block = matrix_ref.shape[1]

    def basis_copy(target):
        return pltpu.make_async_remote_copy(
            src_ref=basis_ref,
            dst_ref=basis.at[pl.ds(chip * vectors, vectors)],
            send_sem=basis_send.at[target],
            recv_sem=basis_recv.at[chip],
            device_id={"row": CORES * col + core, "col": target},
            device_id_type=MESH,
        )

    def basis_own():
        return pltpu.make_async_copy(
            basis_ref, basis.at[pl.ds(chip * vectors, vectors)], basis_recv.at[chip]
        )

    def rows_own(step):
        return pltpu.make_async_copy(
            matrix_ref.at[:, pl.ds(step * width, width)],
            rows.at[step, pl.ds(core * depth, depth)],
            rows_local.at[step],
        )

    def rows_peer(step, owner):
        return pltpu.make_async_remote_copy(
            src_ref=matrix_ref.at[:, pl.ds(step * width, width)],
            dst_ref=rows.at[step, pl.ds(owner * depth, depth)],
            send_sem=rows_send.at[step],
            recv_sem=rows_recv.at[step],
            device_id={"row": CORES * chip + 1 - core, "col": col},
            device_id_type=MESH,
        )

    def sum_copy(source, owner, slot, step, towards):
        return pltpu.make_async_remote_copy(
            src_ref=source,
            dst_ref=sums.at[slot, step],
            send_sem=sum_send.at[owner, step],
            recv_sem=sum_recv.at[slot, step],
            device_id={"row": CORES * towards + core, "col": col},
            device_id_type=MESH,
        )

    def part_of(step, owner):
        return part.at[step, pl.ds(owner * vectors, vectors)]

    def send_up(source, owner, step):
        sum_copy(source, owner, owner, step, chip + 1).start()

    def send_down(source, owner, step):
        slot = jnp.where(owner == chip - 1, chips, owner)
        sum_copy(source, owner, slot, step, chip - 1).start()

    def sum_wait(slot, step):
        neighbour = jnp.where(chip == 0, 1, chip - 1)
        sum_copy(sums.at[slot, step], 0, slot, step, neighbour).wait_recv()

    def out_at(step, owner):
        return out_ref.at[:, pl.ds(owner * block + step * width, width)]

    def out_copy(step, target):
        return pltpu.make_async_remote_copy(
            src_ref=part_of(step, chip),
            dst_ref=out_at(step, col),
            send_sem=out_send.at[target, step],
            recv_sem=out_recv.at[col, step],
            device_id={"row": row, "col": target},
            device_id_type=MESH,
        )

    def out_wait(step, source):
        pltpu.make_async_remote_copy(
            src_ref=part_of(step, chip),
            dst_ref=out_at(step, source),
            send_sem=out_send.at[source, step],
            recv_sem=out_recv.at[source, step],
            device_id={"row": row, "col": source},
            device_id_type=MESH,
        ).wait_recv()

    def out_own(step):
        return pltpu.make_async_copy(part_of(step, chip), out_at(step, col), out_recv.at[col, step])

    for shift in range(cols):
        target = lax.rem(col + shift, cols)
        if shift:
            basis_copy(target).start()
        else:
            pl.when(chip == col)(lambda: basis_own().start())
            pl.when(chip != col)(lambda: basis_copy(col).start())

    @pl.loop(0, chunks)
    def _(step):
        rows_peer(step, core).start()
        rows_own(step).start()

    for source in range(chips):
        pltpu.make_async_copy(
            basis_ref, basis.at[pl.ds(source * vectors, vectors)], basis_recv.at[source]
        ).wait()
    high, low = split_parts(basis[...])
    count = chips * vectors
    halves[:count] = high
    halves[count:] = low

    tile = min(256, width)

    @pl.loop(0, chunks)
    def _(step):
        rows_own(step).wait()
        rows_peer(step, 1 - core).wait_recv()

        @pl.loop(0, width // tile)
        def _(at):
            lanes = pl.ds(pl.multiple_of(at * tile, tile), tile)
            right, rest = split_parts(rows[step, :, lanes])
            inner = CORES * depth
            both = jnp.dot(halves[:, :inner], right, preferred_element_type=jnp.float32)
            third = jnp.dot(halves[:count, :inner], rest, preferred_element_type=jnp.float32)
            part[step, :, lanes] = both[:count] + (both[count:] + third)

        @pl.when(chip == 0)
        def _():
            for owner in range(chips - 1, 0, -1):
                send_up(part_of(step, owner), owner, step)

        @pl.when(chip == chips - 1)
        def _():
            for owner in range(chips - 1):
                send_down(part_of(step, owner), owner, step)

    def add(step, slot, owner):
        at = pl.ds(pl.multiple_of(owner * vectors, vectors), vectors)
        return sums[slot, step] + part[step, at]

    @pl.loop(0, chunks)
    def _(step):
        for owner in range(chips - 1, 0, -1):

            @pl.when((chip > 0) & (chip < owner))
            def _():
                sum_wait(owner, step)
                sums[owner, step] = add(step, owner, owner)
                send_up(sums.at[owner, step], owner, step)

            down = chips - 1 - owner

            @pl.when((chip < chips - 1) & (chip > down))
            def _():
                sum_wait(down, step)
                sums[down, step] = add(step, down, down)
                send_down(sums.at[down, step], down, step)

        mine = pl.ds(pl.multiple_of(chip * vectors, vectors), vectors)

        @pl.when(chip > 0)
        def _():
            sum_wait(chip, step)
            part[step, mine] = sums[chip, step] + part[step, mine]

        @pl.when(chip < chips - 1)
        def _():
            sum_wait(chips, step)
            part[step, mine] = sums[chips, step] + part[step, mine]

        for shift in range(1, cols):
            out_copy(step, lax.rem(col + shift, cols)).start()
        out_own(step).start()

    for shift in range(cols):
        target = lax.rem(col + shift, cols)
        if shift:
            basis_copy(target).wait_send()
        else:
            pl.when(chip != col)(lambda: basis_copy(col).wait_send())

    @pl.loop(0, chunks)
    def _(step):
        rows_peer(step, core).wait_send()
        for owner in range(chips):
            neighbour = jnp.where(chip == 0, 1, chip - 1)

            @pl.when(owner != chip)
            def _():
                sum_copy(part_of(step, owner), owner, owner, step, neighbour).wait_send()

        for shift in range(1, cols):
            other = lax.rem(col + shift, cols)
            out_copy(step, other).wait_send()
            out_wait(step, other)
        out_own(step).wait()


def solution(mesh):
    chips, cols = mesh.shape["row"] // CORES, mesh.shape["col"]

    def per_device(matrix, range_basis):
        depth, block = matrix.shape
        inner, vectors = range_basis.shape
        assert chips == cols and inner == CORES * depth
        padded = -(-inner // 128) * 128
        width = block // CHUNKS
        mine = jnp.pad(range_basis.T, ((0, 0), (0, padded - inner)))
        count = chips * vectors
        dma = pltpu.SemaphoreType.DMA
        return pl.pallas_call(
            lambda *refs: kernel(chips, cols, *refs),
            out_shape=jax.ShapeDtypeStruct((vectors, cols * block), jnp.float32),
            in_specs=[
                pl.BlockSpec(memory_space=pltpu.VMEM),
                pl.BlockSpec(memory_space=pl.ANY),
            ],
            out_specs=pl.BlockSpec(memory_space=pl.ANY),
            scratch_shapes=[
                pltpu.VMEM((count, padded), jnp.float32),
                pltpu.VMEM((2 * count, padded), jnp.bfloat16),
                pltpu.VMEM((CHUNKS, inner, width), jnp.float32),
                pltpu.VMEM((CHUNKS, count, width), jnp.float32),
                pltpu.VMEM((chips + 1, CHUNKS, vectors, width), jnp.float32),
                dma((cols,)),
                dma((chips,)),
                dma((CHUNKS,)),
                dma((CHUNKS,)),
                dma((CHUNKS,)),
                dma((chips, CHUNKS)),
                dma((chips + 1, CHUNKS)),
                dma((cols, CHUNKS)),
                dma((cols, CHUNKS)),
            ],
            compiler_params=pltpu.CompilerParams(
                has_side_effects=True, vmem_limit_bytes=66_000_000
            ),
        )(mine, matrix)

    return jax.shard_map(
        per_device,
        mesh=mesh,
        in_specs=(P("row", "col"), P("col", "row")),
        out_specs=P("row", None),
        check_vma=False,
    )
```

time: 446 us -> 298 us (0.67)
  waiting for transfers between devices: 368 us -> 0 us
  Pallas kernels: 0 us -> 286 us
  blocking collectives: 28.5 us -> 0 us
  matrix products: 25.4 us -> 0 us
  between operations: 13.4 us -> 0.01 us
    pallas_call x0 -> x1, Pallas kernels: none -> 286 us  [per_device(): pl.pallas_call(lambda *refs: kernel(chips, cols, *refs), out_shape=jax.Sh...]
    reduce_scatter x1 -> x0, waiting for transfers between devices: 245 us -> none  [per_device(): lax.psum_scatter(project(local_basis, matrix), 'row', scatter_dimension=0...]
    all_gather x1 -> x0, waiting for transfers between devices: 123 us -> none  [per_device(): return lax.all_gather(owned_rows, 'col', axis=1, tiled=True)]
    dot_general x1 -> x0, matrix products: 25.4 us -> none  [project(): lax.dot_general(left, right, (((0,), (0,)), ((), ())), precision=lax.Prec...]
    all_to_all x1 -> x0, blocking collectives: 17.2 us -> none  [per_device(): lax.all_to_all(row_panel, 'row', split_axis=0, concat_axis=1, tiled=True)]
    all_gather x1 -> x0, blocking collectives: 11.3 us -> none  [per_device(): row_panel = lax.all_gather(range_basis, 'col', axis=0, tiled=True)]
  transfers between devices with their start and end apart: 2 -> 0, of which waited for: 2 -> 0; matrix products, arithmetic and copies ran while one was open for 0% -> 0% of each run, Pallas kernels for 0% -> 0%
where the time goes in v1:
time: 298 us; the launch traced here: 297 us
  Pallas kernels  286 us (96%)
  local copies, waits for them, and re-layouts  11.7 us (4%)
    pallas_call x1, Pallas kernels, per_device(): pl.pallas_call(lambda *refs: kernel(chips, cols, *refs), out_shape=jax.Sh...  286 us
    unnamed x1, local copies, waits for them, and re-layouts  10.2 us

profile of v1, /device:TPU:0, one launch (start us, length us, event | category | flops | bytes accessed | tf_op | source)
XLA Modules:
  0.0 297.4 jit_solution(16345758936241186131)
XLA Ops:
  0.0 1.5 pad.4.refs_0_
  1.5 285.7 %shard_map.28 = f32[48,65536]{1,0:T(8,128)} custom-call(f32[48,512]{1,0:T(8,128)} %pad.4.refs_0_, f32[216,16384]{1,0:T(8,128)} %refs_1_.1), custom_call_target="tpu_custom_call" | custom-call | tf_op jit(solution)/shard_map/pallas_call | solution.py:233
  287.2 10.2 %copy.4 = f32[48,65536]{1,0:T(8,128)} copy(f32[48,65536]{1,0:T(8,128)} %shard_map.28) | data formatting | bytes 25165824
